TPU v7x, 32 devices: a whole 2x2x4 slice. The times are simulated.
32 devices in a mesh: groups: 2 (over x), dp: 2 (over core), seq: 8 (over z, y).
Axes of the slice: x: 2, y: 2, z: 4, core: 2. Of those that a mesh axis runs over, the one named last changes fastest.
Arguments:
- history: bfloat16 [8, 768, 1024], P(('groups', 'dp'), 'seq'), parts along dimension 0, may hold values from -20 to 20
- candidates: bfloat16 [4, 512, 1024], P(('groups', 'dp'), 'seq'), parts along dimension 0, may hold values from -6 to 6
- lengths: int32 [8], P(('groups', 'dp')), parts along dimension 0, may hold values from 96 to 768
- assignment: int32 [4, 512], P(('groups', 'dp'), 'seq'), parts along dimension 0, may hold values from 0 to 1, as said below
- weight_in: bfloat16 [1024, 4096], replicated, may hold values from -0.1875 to 0.1875
- weight_out: bfloat16 [1024, 1024], replicated, may hold values from -0.1875 to 0.1875
- gain_in: float32 [1024], replicated, may hold values from 0.25 to 1.75
- gain_attn: float32 [1024], replicated, may hold values from 0.25 to 1.75
Outputs:
- history_out: bfloat16 [8, 768, 1024], P(('groups', 'dp'), 'seq'), parts along dimension 0
- candidate_out: bfloat16 [4, 512, 1024], P(('groups', 'dp'), 'seq'), parts along dimension 0
There are 2 independent parts, one for each index of `groups`. A program takes and returns all parts, laid end to end along the dimension named above; an argument that names none is the same for every part. Nothing has to cross between parts.
Inputs may be any that keep to these rules, and one draw needn't show every extreme that they name: `assignment`: of the 64 candidates of one device, at most 40 belong to either history; in every dp index some device has exactly 40 of the first and another exactly 40 of the second.
All inputs are finite; a program needn't handle non-finite values.
Results may differ from a plain program's by a relative error of at most 0.0075.
Values may be sent and summed in bfloat16 or wider, within the bound.
A program may use at most 192 MiB of HBM per device.

v0:
```python
import math

import jax
import jax.numpy as jnp
from jax import lax
from jax.sharding import PartitionSpec as P

H = 16
HD = 64
CAP = 40


def rms_apply(values, gain):
    return values * lax.rsqrt(jnp.mean(values * values, axis=-1, keepdims=True) + 1e-06) * gain


def self_item(packed):
    query, keys, values, valid = packed
    length = keys.shape[0]
    score_scale = HD ** (-0.5)
    block_rows = math.gcd(length, 512)
    key_positions = jnp.arange(length, dtype=jnp.int32)

    def query_part(inner):
        query_block, first_row = inner
        scores = jnp.dot(query_block, keys.T, preferred_element_type=jnp.float32) * score_scale
        row_positions = first_row + jnp.arange(block_rows, dtype=jnp.int32)
        allowed = (key_positions[None, :] <= row_positions[:, None]) & (
            key_positions[None, :] < valid
        )
        weights = jnp.where(allowed, jax.nn.silu(scores), 0.0).astype(jnp.bfloat16)
        return jnp.dot(weights, values, preferred_element_type=jnp.float32).astype(jnp.bfloat16)

    starts = jnp.arange(length // block_rows, dtype=jnp.int32) * block_rows
    result = lax.map(query_part, (query.reshape(length // block_rows, block_rows, HD), starts))
    return result.reshape(length, HD)


def cand_item(packed):
    queries, keys, values, valid = packed
    cand_total = queries.shape[0]
    score_scale = HD ** (-0.5)
    block_rows = math.gcd(cand_total, 1024)
    key_positions = jnp.arange(keys.shape[0], dtype=jnp.int32)

    def cand_part(query_block):
        scores = jnp.dot(query_block, keys.T, preferred_element_type=jnp.float32) * score_scale
        weights = jnp.where(key_positions[None, :] < valid, jax.nn.silu(scores), 0.0).astype(
            jnp.bfloat16
        )
        return jnp.dot(weights, values, preferred_element_type=jnp.float32).astype(jnp.bfloat16)

    result = lax.map(cand_part, queries.reshape(cand_total // block_rows, block_rows, HD))
    return result.reshape(cand_total, HD)


def place_windows(windows, cand_count, window_rows, inverse):
    first = jnp.pad(windows[0], ((0, cand_count - window_rows), (0, 0), (0, 0)))
    second = jnp.pad(windows[1], ((cand_count - window_rows, 0), (0, 0), (0, 0)))
    return (first + second)[inverse]


def per_device(history, candidates, lengths, assignment, weight_in, weight_out, gain_in, gain_attn):
    seq_devices = lax.axis_size("seq")
    hist_local, tok_share, model_width = history.shape
    item_count = hist_local * H
    items_local = item_count // seq_devices
    length = tok_share * seq_devices
    hist_float = history.astype(jnp.float32)
    normed = (
        rms_apply(hist_float, gain_in)
        .astype(jnp.bfloat16)
        .reshape(hist_local * tok_share, model_width)
    )
    projected = jnp.dot(normed, weight_in, preferred_element_type=jnp.float32)
    gate = jax.nn.silu(projected[:, :model_width]).astype(jnp.bfloat16)
    query = projected[:, model_width : 2 * model_width].astype(jnp.bfloat16)
    keys = projected[:, 2 * model_width : 3 * model_width].astype(jnp.bfloat16)
    values = projected[:, 3 * model_width :].astype(jnp.bfloat16)

    def to_items(matrix):
        return (
            matrix.reshape(hist_local, tok_share, H, HD)
            .transpose(0, 2, 1, 3)
            .reshape(item_count, tok_share * HD)
        )

    exchanged = (
        lax.all_to_all(to_items(query), "seq", split_axis=0, concat_axis=1, tiled=True),
        lax.all_to_all(to_items(keys), "seq", split_axis=0, concat_axis=1, tiled=True),
        lax.all_to_all(to_items(values), "seq", split_axis=0, concat_axis=1, tiled=True),
    )
    heads_query = exchanged[0].reshape(items_local, length, HD)
    heads_keys = exchanged[1].reshape(items_local, length, HD)
    heads_values = exchanged[2].reshape(items_local, length, HD)
    first_item = lax.axis_index("seq") * items_local
    item_hist = (first_item + jnp.arange(items_local, dtype=jnp.int32)) // H
    members = jnp.arange(hist_local, dtype=jnp.int32)
    item_valid = jnp.sum(
        jnp.where(item_hist[:, None] == members[None, :], lengths[None, :], 0), axis=1
    )
    attended = lax.map(self_item, (heads_query, heads_keys, heads_values, item_valid))
    returned = lax.all_to_all(
        attended.reshape(items_local, length * HD), "seq", split_axis=1, concat_axis=0, tiled=True
    )
    returned = (
        returned.reshape(hist_local, H, tok_share, HD)
        .transpose(0, 2, 1, 3)
        .reshape(hist_local * tok_share, model_width)
    )
    gated_rows = (
        rms_apply(returned.astype(jnp.float32), gain_attn) * gate.astype(jnp.float32)
    ).astype(jnp.bfloat16)
    history_out = hist_float.reshape(hist_local * tok_share, model_width) + jnp.dot(
        gated_rows, weight_out, preferred_element_type=jnp.float32
    )
    history_out = history_out.astype(jnp.bfloat16).reshape(hist_local, tok_share, model_width)
    cand_rows = candidates[0]
    cand_count = cand_rows.shape[0]
    window_rows = CAP
    owner = assignment[0]
    cand_float = cand_rows.astype(jnp.float32)
    cand_normed = rms_apply(cand_float, gain_in).astype(jnp.bfloat16)
    cand_proj = jnp.dot(
        cand_normed, weight_in[:, : 2 * model_width], preferred_element_type=jnp.float32
    )
    cand_gate = jax.nn.silu(cand_proj[:, :model_width]).astype(jnp.bfloat16)
    cand_query = cand_proj[:, model_width:].astype(jnp.bfloat16).reshape(cand_count, H, HD)
    order = jnp.argsort(owner * cand_count + jnp.arange(cand_count, dtype=jnp.int32))
    inverse = jnp.argsort(order)
    sorted_query = cand_query[order]
    sorted_owner = owner[order]
    window_starts = [0, cand_count - window_rows]
    window_list = []
    for member in range(hist_local):
        start = window_starts[member]
        rows_here = sorted_query[start : start + window_rows]
        mine = sorted_owner[start : start + window_rows] == member
        window_list.append(jnp.where(mine[:, None, None], rows_here, jnp.zeros_like(rows_here)))
    window_query = jnp.stack(window_list)
    outgoing = window_query.transpose(0, 2, 1, 3).reshape(item_count, window_rows * HD)
    incoming = lax.all_to_all(outgoing, "seq", split_axis=0, concat_axis=1, tiled=True)
    incoming = incoming.reshape(items_local, seq_devices * window_rows, HD)
    results = lax.map(cand_item, (incoming, heads_keys, heads_values, item_valid))
    back_home = lax.all_to_all(
        results.reshape(items_local, seq_devices * window_rows * HD),
        "seq",
        split_axis=1,
        concat_axis=0,
        tiled=True,
    )
    back_home = (
        back_home.reshape(hist_local, H, window_rows, HD).transpose(0, 2, 1, 3).astype(jnp.float32)
    )
    cross_attended = (
        place_windows(back_home, cand_count, window_rows, inverse)
        .astype(jnp.bfloat16)
        .reshape(cand_count, model_width)
    )
    cand_gated = (
        rms_apply(cross_attended.astype(jnp.float32), gain_attn) * cand_gate.astype(jnp.float32)
    ).astype(jnp.bfloat16)
    candidate_out = (
        cand_float + jnp.dot(cand_gated, weight_out, preferred_element_type=jnp.float32)
    ).astype(jnp.bfloat16)
    return (history_out, candidate_out[None])


def solution(mesh):
    in_specs = (
        P(("groups", "dp"), "seq", None),
        P(("groups", "dp"), "seq", None),
        P(("groups", "dp")),
        P(("groups", "dp"), "seq"),
        P(),
        P(),
        P(),
        P(),
    )
    out_specs = (P(("groups", "dp"), "seq", None), P(("groups", "dp"), "seq", None))
    return jax.shard_map(
        per_device, mesh=mesh, in_specs=in_specs, out_specs=out_specs, check_vma=False
    )
```

profile of v0, /device:TPU:0, one launch (start us, length us, event | category | flops | bytes accessed | tf_op | source)
XLA Modules:
  0.0 198.5 jit_solution(17433720871256379200)
XLA Ops:
  1.5 2.0 %sort.31 = (s32[64]{0:T(128)}, s32[64]{0:T(128)S(1)}) sort(s32[64]{0:T(128)S(1)} %iota_add_fusion.1, s32[64]{0:T(128)S(1)} %iota.37), dimensions={0}, to_apply=%region_8.9 | sort | flops 384 | bytes 1024 | tf_op jit(solution)/shard_map/jit(argsort)/sort | solution.py:129
  4.6 3.2 %fusion.37 = f32[64,2048]{1,0:T(8,128)S(1)} fusion(bf16[1024,4096]{1,0:T(8,128)(2,1)} %param.20, bf16[1,64,1024]{2,1,0:T(8,128)(2,1)} %param.17, f32[1024]{0:T(1024)} %param.22, f32[64]{0:T(128)S(1)} %add_rsqrt_fusion.3), kind=kOutput, calls=%fused_computation.50 | convolution fusion | flops 268697600 | bytes 4854016 | tf_op jit(solution)/shard_map/dot_general | solution.py:124
  11.5 7.3 %all-to-all-start.4 = ((bf16[8,4,2560]{2,1,0:T(4,128)(2,1)}), bf16[8,4,2560]{2,1,0:T(4,128)(2,1)}, u32[]{:S(2)}, u32[]{:S(2)}) async-start(bf16[8,4,2560]{2,1,0:T(4,128)(2,1)} %all_to_all.79), calls=%async_computation.4 | async-start | bytes 327680 | tf_op jit(solution)/shard_map/all_to_all | solution.py:142
  19.1 6.9 %fusion.62 = (bf16[192,4096]{1,0:T(8,128)(2,1)S(1)}, f32[192,4096]{1,0:T(8,128)}) fusion(bf16[192,1024]{1,0:T(8,128)(2,1)S(1)} %bitcast.139, bf16[1024,4096]{1,0:T(8,128)(2,1)} %param.20), kind=kOutput, calls=%fused_computation.113 | convolution fusion | flops 1611399168 | bytes 13500416 | tf_op jit(solution)/shard_map/dot_general | solution.py:75
  28.1 1.3 all_to_all.71
  29.4 6.0 %all-to-all-start.1 = ((bf16[8,4,6144]{2,1,0:T(4,128)(2,1)}), bf16[8,4,6144]{2,1,0:T(4,128)(2,1)}, u32[]{:S(2)}, u32[]{:S(2)}) async-start(bf16[8,4,6144]{2,1,0:T(4,128)(2,1)} %all_to_all.71), calls=%async_computation.1 | async-start | bytes 786432 | tf_op jit(solution)/shard_map/all_to_all | solution.py:90
  37.4 1.3 all_to_all.74
  38.7 7.9 %all-to-all-done.1 = bf16[8,4,6144]{2,1,0:T(4,128)(2,1)} async-done(((bf16[8,4,6144]{2,1,0:T(4,128)(2,1)}), bf16[8,4,6144]{2,1,0:T(4,128)(2,1)}, u32[]{:S(2)}, u32[]{:S(2)}) %all-to-all-start.1) | async-done | bytes 393248 | tf_op jit(solution)/shard_map/all_to_all | solution.py:90
  46.6 4.1 %all-to-all-start.2 = ((bf16[8,4,6144]{2,1,0:T(4,128)(2,1)}), bf16[8,4,6144]{2,1,0:T(4,128)(2,1)}, u32[]{:S(2)}, u32[]{:S(2)}) async-start(bf16[8,4,6144]{2,1,0:T(4,128)(2,1)} %all_to_all.74), calls=%async_computation.2 | async-start | bytes 786432 | tf_op jit(solution)/shard_map/all_to_all | solution.py:91
  50.7 2.0 %sort.32 = (s32[64]{0:T(128)}, s32[64]{0:T(128)S(1)}) sort(s32[64]{0:T(128)S(1)} %get-tuple-element.151, s32[64]{0:T(128)S(1)} %iota.38), dimensions={0}, to_apply=%region_14.15 | sort | flops 384 | bytes 1024 | tf_op jit(solution)/shard_map/jit(argsort)/sort | solution.py:130
  54.8 1.3 all_to_all.68
  58.1 1.2 copy.67
  60.1 1.7 all-to-all-done.2
  61.9 4.2 %all-to-all-start = ((bf16[8,4,6144]{2,1,0:T(4,128)(2,1)}), bf16[8,4,6144]{2,1,0:T(4,128)(2,1)}, u32[]{:S(2)}, u32[]{:S(2)}) async-start(bf16[8,4,6144]{2,1,0:T(4,128)(2,1)} %all_to_all.68), calls=%async_computation | async-start | bytes 786432 | tf_op jit(solution)/shard_map/all_to_all | solution.py:89
  67.3 1.7 reshape.190
  68.9 32.8 %while.46 = (s32[]{:T(128)}, bf16[4,320,64]{2,1,0:T(8,128)(2,1)}, bf16[4,320,64]{2,1,0:T(8,128)(2,1)}, bf16[4,768,64]{2,1,0:T(8,128)(2,1)S(1)}, s32[4]{0:T(128)S...) while((s32[]{:T(128)}, bf16[4,320,64]{2,1,0:T(8,128)(2,1)}, ...), condition=%wide.region_13.14_spmd, body=%wide.region_10.13_spmd.sunk | while | flops 12931844 | bytes 1027586 | solution.py:144
  71.4 5.1 %while.48 = (s32[]{:T(128)}, bf16[5,64,64]{2,1,0:T(8,128)(2,1)S(1)}, s32[]{:T(128)}, bf16[5,64,64]{2,1,0:T(8,128)(2,1)S(1)}, bf16[768,64]{1,0:T(8,128)(2,1)S(1)}, /*index=5*/bf16[768,64]{1,0:T(8,128)(2,1)S(1)}, s32[]{:T(128)}) while((s32[]{:T(128)}, bf16[5,64,64]{2,1,0:T(8,128)(2,1)S(1)}, s32[]{:T(128)}, ...), condition=%wide.region_12.12_spmd.clone, body=%wide.region_11.11_spmd.clone.sunk | while | flops 12931842 | bytes 428881 | solution.py:53
  79.6 5.1 %while.48 = (s32[]{:T(128)}, bf16[5,64,64]{2,1,0:T(8,128)(2,1)S(1)}, s32[]{:T(128)}, bf16[5,64,64]{2,1,0:T(8,128)(2,1)S(1)}, bf16[768,64]{1,0:T(8,128)(2,1)S(1)}, /*index=5*/bf16[768,64]{1,0:T(8,128)(2,1)S(1)}, s32[]{:T(128)}) while((s32[]{:T(128)}, bf16[5,64,64]{2,1,0:T(8,128)(2,1)S(1)}, s32[]{:T(128)}, ...), condition=%wide.region_12.12_spmd.clone, body=%wide.region_11.11_spmd.clone.sunk | while | flops 12931842 | bytes 428881 | solution.py:53
  87.8 5.1 %while.48 = (s32[]{:T(128)}, bf16[5,64,64]{2,1,0:T(8,128)(2,1)S(1)}, s32[]{:T(128)}, bf16[5,64,64]{2,1,0:T(8,128)(2,1)S(1)}, bf16[768,64]{1,0:T(8,128)(2,1)S(1)}, /*index=5*/bf16[768,64]{1,0:T(8,128)(2,1)S(1)}, s32[]{:T(128)}) while((s32[]{:T(128)}, bf16[5,64,64]{2,1,0:T(8,128)(2,1)S(1)}, s32[]{:T(128)}, ...), condition=%wide.region_12.12_spmd.clone, body=%wide.region_11.11_spmd.clone.sunk | while | flops 12931842 | bytes 428881 | solution.py:53
  96.0 5.1 %while.48 = (s32[]{:T(128)}, bf16[5,64,64]{2,1,0:T(8,128)(2,1)S(1)}, s32[]{:T(128)}, bf16[5,64,64]{2,1,0:T(8,128)(2,1)S(1)}, bf16[768,64]{1,0:T(8,128)(2,1)S(1)}, /*index=5*/bf16[768,64]{1,0:T(8,128)(2,1)S(1)}, s32[]{:T(128)}) while((s32[]{:T(128)}, bf16[5,64,64]{2,1,0:T(8,128)(2,1)S(1)}, s32[]{:T(128)}, ...), condition=%wide.region_12.12_spmd.clone, body=%wide.region_11.11_spmd.clone.sunk | while | flops 12931842 | bytes 428881 | solution.py:53
  101.7 1.2 all_to_all.82
  103.7 6.0 %all-to-all-start.5 = ((bf16[4,8,2560]{2,0,1:T(4,128)(2,1)}), bf16[4,8,2560]{2,0,1:T(4,128)(2,1)}, u32[]{:S(2)}, u32[]{:S(2)}) async-start(bf16[4,8,2560]{2,0,1:T(4,128)(2,1)} %copy.76), calls=%async_computation.5 | async-start | bytes 327680 | tf_op jit(solution)/shard_map/all_to_all | solution.py:145
  110.9 1.7 reshape.186
  112.6 55.4 %while.44 = (s32[]{:T(128)}, bf16[4,768,64]{2,1,0:T(8,128)(2,1)}, bf16[4,768,64]{2,1,0:T(8,128)(2,1)}, bf16[4,768,64]{2,1,0:T(8,128)(2,1)S(1)}, s32[4]{0:T(128)S...) while((s32[]{:T(128)}, bf16[4,768,64]{2,1,0:T(8,128)(2,1)}, ...), condition=%wide.region_5.6_spmd, body=%wide.region_2.5_spmd.sunk | while | flops 52118532 | bytes 1578542 | solution.py:102
  115.1 9.6 %while.47 = (s32[]{:T(128)}, bf16[3,256,64]{1,2,0:T(8,128)(2,1)}, s32[3]{0:T(128)S(1)}, s32[]{:T(128)}, bf16[3,256,64]{2,1,0:T(8,128)(2,1)S(1)}, /*index=5*/bf16...) while((s32[]{:T(128)}, bf16[3,256,64]{1,2,0:T(8,128)(2,1)}, ...), condition=%wide.region_4.4_spmd.clone.clone, body=%wide.region_3.3_spmd.clone.clone.sunk | while | flops 52118528 | bytes 496489 | solution.py:35
  117.0 1.3 fusion.86
  120.2 1.3 fusion.86
  123.4 1.3 fusion.86
  128.9 9.6 %while.47 = (s32[]{:T(128)}, bf16[3,256,64]{1,2,0:T(8,128)(2,1)}, s32[3]{0:T(128)S(1)}, s32[]{:T(128)}, bf16[3,256,64]{2,1,0:T(8,128)(2,1)S(1)}, /*index=5*/bf16...) while((s32[]{:T(128)}, bf16[3,256,64]{1,2,0:T(8,128)(2,1)}, ...), condition=%wide.region_4.4_spmd.clone.clone, body=%wide.region_3.3_spmd.clone.clone.sunk | while | flops 52118528 | bytes 496489 | solution.py:35
  130.9 1.3 fusion.86
  134.1 1.3 fusion.86
  137.3 1.3 fusion.86
  142.8 9.6 %while.47 = (s32[]{:T(128)}, bf16[3,256,64]{1,2,0:T(8,128)(2,1)}, s32[3]{0:T(128)S(1)}, s32[]{:T(128)}, bf16[3,256,64]{2,1,0:T(8,128)(2,1)S(1)}, /*index=5*/bf16...) while((s32[]{:T(128)}, bf16[3,256,64]{1,2,0:T(8,128)(2,1)}, ...), condition=%wide.region_4.4_spmd.clone.clone, body=%wide.region_3.3_spmd.clone.clone.sunk | while | flops 52118528 | bytes 496489 | solution.py:35
  144.7 1.3 fusion.86
  147.9 1.3 fusion.86
  151.1 1.3 fusion.86
  156.7 9.6 %while.47 = (s32[]{:T(128)}, bf16[3,256,64]{1,2,0:T(8,128)(2,1)}, s32[3]{0:T(128)S(1)}, s32[]{:T(128)}, bf16[3,256,64]{2,1,0:T(8,128)(2,1)S(1)}, /*index=5*/bf16...) while((s32[]{:T(128)}, bf16[3,256,64]{1,2,0:T(8,128)(2,1)}, ...), condition=%wide.region_4.4_spmd.clone.clone, body=%wide.region_3.3_spmd.clone.clone.sunk | while | flops 52118528 | bytes 496489 | solution.py:35
  158.6 1.3 fusion.86
  161.8 1.3 fusion.86
  165.0 1.3 fusion.86
  168.0 1.8 all_to_all.77
  170.8 6.0 %all-to-all-start.3 = ((bf16[4,8,6144]{2,0,1:T(4,128)(2,1)}), bf16[4,8,6144]{2,0,1:T(4,128)(2,1)S(1)}, u32[]{:S(2)}, u32[]{:S(2)}) async-start(bf16[4,8,6144]{2,0,1:T(4,128)(2,1)} %copy.71), calls=%async_computation.3 | async-start | bytes 786432 | tf_op jit(solution)/shard_map/all_to_all | solution.py:103
  179.7 2.1 %fusion.41 = bf16[1,64,1024]{2,1,0:T(8,128)(2,1)} fusion(bf16[1024,1024]{1,0:T(8,128)(2,1)S(1)} %copy-done, f32[64,1024]{1,0:T(8,128)S(1)} %reshape.196, f32[64,2048]{1,0:T(8,128)} %copy-done.5, bf16[1,64,1024]{2,1,0:T(8,128)(2,1)S(1)} %copy-done.4, f32[1024]{0:T(1024)S(1)} %copy-done.7, f32[64]{0:T(128)S(1)} %add_rsqrt_fusion.2), kind=kOutput, calls=%fused_computation.56 | convolution fusion | flops 135069696 | bytes 2887936 | tf_op jit(solution)/shard_map/dot_general | solution.py:164
  181.8 4.8 %all-to-all-done.3 = bf16[4,8,6144]{2,0,1:T(4,128)(2,1)S(1)} async-done(((bf16[4,8,6144]{2,0,1:T(4,128)(2,1)}), bf16[4,8,6144]{2,0,1:T(4,128)(2,1)S(1)}, u32[]{:S(2)}, u32[]{:S(2)}) %all-to-all-start.3) | async-done | bytes 393248 | tf_op jit(solution)/shard_map/all_to_all | solution.py:103
  186.7 1.9 reshape.198
  188.6 3.5 %copy.78 = f32[2,96,16,64]{3,2,1,0:T(8,128)} copy(f32[2,96,16,64]{3,1,2,0:T(8,128)} %bitcast.136) | data formatting | bytes 1572864 | tf_op jit(solution)/shard_map/convert_element_type | solution.py:112
  192.1 2.7 %reshape.226 = f32[192,1024]{1,0:T(8,128)} reshape(f32[2,96,16,64]{3,2,1,0:T(8,128)} %copy.78) | data formatting | bytes 1572864 | tf_op jit(solution)/shard_map/convert_element_type | solution.py:112
  195.7 2.8 %fusion.39 = bf16[192,1024]{1,0:T(8,128)(2,1)} fusion(bf16[1024,1024]{1,0:T(8,128)(2,1)S(1)} %copy-done, f32[192,1024]{1,0:T(8,128)} %reshape.226, f32[192,4096]{1,0:T(8,128)} %get-tuple-element.268, f32[1024]{0:T(1024)S(1)} %copy-done.7, f32[192]{0:T(256)S(1)} %rsqrt.37, bf16[192,1024]{1,0:T(8,128)(2,1)S(1)} %bitcast.145), kind=kOutput, calls=%fused_computation.53 | convolution fusion | flops 405209088 | bytes 4461312 | tf_op jit(solution)/shard_map/dot_general | solution.py:114
  (202 shorter events, 95.1 us)
Async XLA Ops:
  0.6 179.1 %copy-start = (bf16[1024,1024]{1,0:T(8,128)(2,1)S(1)}, bf16[1024,1024]{1,0:T(8,128)(2,1)}, u32[]{:S(2)}) copy-start(bf16[1024,1024]{1,0:T(8,128)(2,1)} %param.21) | copy-start | bytes 6291460
  4.5 4.9 %copy-start.1 = (s32[1,64]{1,0:T(1,128)S(1)}, s32[1,64]{1,0:T(1,128)}, u32[]{:S(2)}) copy-start(s32[1,64]{1,0:T(1,128)} %param.19) | copy-start | bytes 772
  7.8 0.8 copy-start.5
  8.6 10.2 %copy-start.2 = (bf16[2,96,1024]{2,1,0:T(8,128)(2,1)S(1)}, bf16[2,96,1024]{2,1,0:T(8,128)(2,1)}, u32[]{:S(2)}) copy-start(bf16[2,96,1024]{2,1,0:T(8,128)(2,1)} %param.16) | copy-start | bytes 1179652
  8.6 10.4 %copy-start.6 = (f32[1024]{0:T(1024)S(1)}, f32[1024]{0:T(1024)}, u32[]{:S(2)}) copy-start(f32[1024]{0:T(1024)} %param.22) | copy-start | bytes 12292
  11.5 17.9 %all-to-all-start.4 = ((bf16[8,4,2560]{2,1,0:T(4,128)(2,1)}), bf16[8,4,2560]{2,1,0:T(4,128)(2,1)}, u32[]{:S(2)}, u32[]{:S(2)}) async-start(bf16[8,4,2560]{2,1,0:T(4,128)(2,1)} %all_to_all.79), calls=%async_computation.4 | async-start | bytes 327680 | tf_op jit(solution)/shard_map/all_to_all | solution.py:142
  29.4 17.2 %all-to-all-start.1 = ((bf16[8,4,6144]{2,1,0:T(4,128)(2,1)}), bf16[8,4,6144]{2,1,0:T(4,128)(2,1)}, u32[]{:S(2)}, u32[]{:S(2)}) async-start(bf16[8,4,6144]{2,1,0:T(4,128)(2,1)} %all_to_all.71), calls=%async_computation.1 | async-start | bytes 786432 | tf_op jit(solution)/shard_map/all_to_all | solution.py:90
  37.4 18.7 %copy-start.8 = (s32[2]{0:T(128)S(1)}, s32[2]{0:T(128)}, u32[]{:S(2)}) copy-start(s32[2]{0:T(128)} %param.18) | copy-start | bytes 28
  46.6 15.3 %all-to-all-start.2 = ((bf16[8,4,6144]{2,1,0:T(4,128)(2,1)}), bf16[8,4,6144]{2,1,0:T(4,128)(2,1)}, u32[]{:S(2)}, u32[]{:S(2)}) async-start(bf16[8,4,6144]{2,1,0:T(4,128)(2,1)} %all_to_all.74), calls=%async_computation.2 | async-start | bytes 786432 | tf_op jit(solution)/shard_map/all_to_all | solution.py:91
  61.9 41.8 %all-to-all-start = ((bf16[8,4,6144]{2,1,0:T(4,128)(2,1)}), bf16[8,4,6144]{2,1,0:T(4,128)(2,1)}, u32[]{:S(2)}, u32[]{:S(2)}) async-start(bf16[8,4,6144]{2,1,0:T(4,128)(2,1)} %all_to_all.68), calls=%async_computation | async-start | bytes 786432 | tf_op jit(solution)/shard_map/all_to_all | solution.py:89
  103.7 67.2 %all-to-all-start.5 = ((bf16[4,8,2560]{2,0,1:T(4,128)(2,1)}), bf16[4,8,2560]{2,0,1:T(4,128)(2,1)}, u32[]{:S(2)}, u32[]{:S(2)}) async-start(bf16[4,8,2560]{2,0,1:T(4,128)(2,1)} %copy.76), calls=%async_computation.5 | async-start | bytes 327680 | tf_op jit(solution)/shard_map/all_to_all | solution.py:145
  170.8 15.8 %all-to-all-start.3 = ((bf16[4,8,6144]{2,0,1:T(4,128)(2,1)}), bf16[4,8,6144]{2,0,1:T(4,128)(2,1)S(1)}, u32[]{:S(2)}, u32[]{:S(2)}) async-start(bf16[4,8,6144]{2,0,1:T(4,128)(2,1)} %copy.71), calls=%async_computation.3 | async-start | bytes 786432 | tf_op jit(solution)/shard_map/all_to_all | solution.py:103
  176.8 2.9 %copy-start.7 = (f32[1024]{0:T(1024)S(1)}, f32[1024]{0:T(1024)}, u32[]{:S(2)}) copy-start(f32[1024]{0:T(1024)} %param.23) | copy-start | bytes 12292
  178.0 1.7 copy-start.4
  188.6 7.1 %copy-start.3 = (bf16[2,96,1024]{2,1,0:T(8,128)(2,1)S(1)}, bf16[2,96,1024]{2,1,0:T(8,128)(2,1)}, u32[]{:S(2)}) copy-start(bf16[2,96,1024]{2,1,0:T(8,128)(2,1)} %param.16) | copy-start | bytes 1179652
where the time goes:
time: 201 us; the launch traced here: 199 us
  local copies, waits for them, and re-layouts  74.7 us (37%)
  matrix products  37.3 us (19%)
  other arithmetic  36.8 us (18%)
  starting transfers between devices  33.6 us (17%)
  waiting for transfers between devices  14.4 us (7%)
    dot_general x12, matrix products, query_part(): jnp.dot(weights, values, preferred_element_type=jnp.float32)  15.2 us
    lt x20, other arithmetic, cand_part(): key_positions[None, :] < valid  12.7 us
    dynamic_slice x12, local copies, waits for them, and re-layouts, per_device(): lax.map(self_item, (heads_query, heads_keys, heads_values, item_valid))  8.53 us
    add x12, other arithmetic, query_part(): row_positions = first_row + jnp.arange(block_rows, dtype=jnp.int32)  8.29 us
    convert_element_type x3, local copies, waits for them, and re-layouts, per_device(): returned.astype(jnp.float32)  8.11 us
    dynamic_slice x12, local copies, waits for them, and re-layouts, self_item(): lax.map(query_part, (query.reshape(length // block_rows, block_rows, HD),...  7.94 us
    all_to_all x1, waiting for transfers between devices, per_device(): lax.all_to_all(to_items(keys), 'seq', split_axis=0, concat_axis=1, tiled=...  7.85 us
    squeeze x8, local copies, waits for them, and re-layouts, per_device(): lax.map(self_item, (heads_query, heads_keys, heads_values, item_valid))  7.62 us
  transfers between devices with their start and end apart: 6, of which 3 were waited for; matrix products, arithmetic and copies ran while one was open for 60% of the time, Pallas kernels for 0%

commit v1 on v0

v1 whole, which is shorter than its diff:
```python
import functools

import jax
import jax.numpy as jnp
from jax import lax
from jax.experimental import pallas as pl
from jax.experimental.pallas import tpu as pltpu
from jax.sharding import PartitionSpec as P

H = 16
CAP = 40
ROW_TILE = 16
MESH = pl.DeviceIdType.MESH
F32 = jnp.float32
BF16 = jnp.bfloat16
KEY, VALUE, CAND, QUERY, BACK, CROSS = range(6)


def dot(a, b, dims=((1,), (0,))):
    return lax.dot_general(a, b, (dims, ((), ())), preferred_element_type=F32)


def silu_half(u):
    return u + u * jnp.tanh(u)


def rms_apply(values, gain):
    return values * lax.rsqrt(jnp.mean(values * values, axis=-1, keepdims=True) + 1e-06) * gain


def layer_kernel(
    seq_devices,
    len_ref,
    hist_ref,
    cand_ref,
    owner_ref,
    gain_in_ref,
    gain_attn_ref,
    w_in_ref,
    w_out_ref,
    hist_out_ref,
    cand_out_ref,
    w_buf,
    wo_buf,
    normed_ref,
    gate_ref,
    cand_gate_ref,
    send_kvq,
    send_c,
    recv_k,
    recv_v,
    recv_q,
    recv_c,
    key_heads,
    value_heads,
    att_ref,
    cross_ref,
    back_ref,
    back_c_ref,
    w_sem,
    send_sem,
    recv_sem,
):
    S = seq_devices
    me = lax.axis_index("seq")
    hists, tokens, width = hist_ref.shape
    cands = cand_ref.shape[0]
    heads_here = hists * H // S
    head_dim = width // H
    W = heads_here * head_dim
    blocks = width // W
    window = recv_c.shape[0] // S
    length = tokens * S
    my_hist = me // blocks

    def weight_copy(part):
        return pltpu.make_async_copy(
            w_in_ref.at[:, pl.ds(part * width, width)], w_buf.at[part], w_sem.at[part]
        )

    for part in (2, 3, 1, 0):
        weight_copy(part).start()
    out_copy = pltpu.make_async_copy(w_out_ref, wo_buf, w_sem.at[4])
    out_copy.start()

    barrier = pltpu.get_barrier_semaphore()
    for step in range(1, S):
        pl.semaphore_signal(
            barrier, inc=1, device_id={"seq": lax.rem(me + step, S)}, device_id_type=MESH
        )

    gain_in = gain_in_ref[...]
    hist_rows = hist_ref[...].reshape(hists * tokens, width).astype(F32)
    normed_ref[...] = rms_apply(hist_rows, gain_in).astype(BF16)
    chunk = max(W, min(width, 256))

    def blocks_of(first, value):
        for sub in range(0, chunk, W):
            yield (first + sub) // W, value[:, sub : sub + W]

    def remote(phase, src, dst, other):
        return pltpu.make_async_remote_copy(
            src_ref=src,
            dst_ref=dst,
            send_sem=send_sem.at[phase, other],
            recv_sem=recv_sem.at[phase, me],
            device_id={"seq": other},
            device_id_type=MESH,
        )

    def arrival(phase, ref, rows, source):
        here = ref.at[pl.ds(source * rows, rows), :]
        return pltpu.make_async_remote_copy(
            src_ref=here,
            dst_ref=here,
            send_sem=send_sem.at[phase, source],
            recv_sem=recv_sem.at[phase, source],
            device_id={"seq": source},
            device_id_type=MESH,
        )

    sent = []

    def scatter(phase, src, dst, rows):
        for step in range(1, S):
            other = lax.rem(me + step, S)
            copy = remote(phase, src(other), dst.at[pl.ds(me * rows, rows), :], other)
            copy.start()
            sent.append(copy)

    def project_and_send(phase, part, slot, dst):
        normed = normed_ref[...]
        for first in range(0, width, chunk):
            value = dot(normed, w_buf[part, :, first : first + chunk]).astype(BF16)
            for block, piece in blocks_of(first, value):
                for n in range(hists):
                    send_kvq[slot, n * blocks + block] = piece[n * tokens : (n + 1) * tokens]
        if phase == KEY:
            pl.semaphore_wait(barrier, S - 1)
        scatter(phase, lambda other: send_kvq.at[slot, other], dst, tokens)
        dst[pl.ds(pl.multiple_of(me * tokens, ROW_TILE), tokens), :] = send_kvq[slot, me]

    weight_copy(2).wait()
    project_and_send(KEY, 2, 0, recv_k)
    weight_copy(3).wait()
    project_and_send(VALUE, 3, 1, recv_v)

    cand_rows = cand_ref[...].astype(F32)
    cand_normed = rms_apply(cand_rows, gain_in).astype(BF16)
    owner = owner_ref[...]
    before = (
        lax.broadcasted_iota(jnp.int32, (cands, cands), 0)
        < lax.broadcasted_iota(jnp.int32, (cands, cands), 1)
    ).astype(F32)
    place = jnp.zeros((1, cands), F32)
    for n in range(hists):
        mine = (owner == n).astype(F32)
        rank = dot(jnp.broadcast_to(mine, (8, cands)), before)[0:1]
        place = place + mine * (rank + n * window)
    picks = (
        lax.broadcasted_iota(jnp.int32, (hists * window, cands), 0).astype(F32) == place
    ).astype(F32).astype(BF16)

    weight_copy(1).wait()
    for first in range(0, width, chunk):
        value = dot(cand_normed, w_buf[1, :, first : first + chunk]).astype(BF16)
        value = dot(picks, value).astype(BF16)
        for block, piece in blocks_of(first, value):
            for n in range(hists):
                send_c[n * blocks + block] = piece[n * window : (n + 1) * window]
    scatter(CAND, lambda other: send_c.at[other], recv_c, window)
    recv_c[pl.ds(pl.multiple_of(me * window, ROW_TILE), window), :] = send_c[me]
    project_and_send(QUERY, 1, 2, recv_q)

    weight_copy(0).wait()
    for first in range(0, width, chunk):
        cols = slice(first, first + chunk)
        wide = w_buf[0, :, cols]
        gate_ref[:, cols] = silu_half(0.5 * dot(normed_ref[...], wide)).astype(BF16)
        cand_gate_ref[:, cols] = silu_half(0.5 * dot(cand_normed, wide)).astype(BF16)

    def wait_all(phase, ref, rows):
        for step in range(1, S):
            arrival(phase, ref, rows, lax.rem(me + S - step, S)).wait_recv()

    lane_head = lax.broadcasted_iota(jnp.int32, (1, W), 1) // head_dim
    score_half = 0.5 * head_dim ** (-0.5)
    wait_all(KEY, recv_k, tokens)
    for t in range(heads_here):
        pick = jnp.where(lane_head == t, score_half, 0.0).astype(BF16)
        key_heads[t] = recv_k[...] * pick
    wait_all(VALUE, recv_v, tokens)
    valid = len_ref[my_hist]
    inside = (lax.broadcasted_iota(jnp.int32, (length, W), 0) < valid).astype(F32).astype(BF16)
    values = recv_v[...] * inside
    for t in range(heads_here):
        pick = (lane_head == t).astype(F32).astype(BF16)
        value_heads[t] = values * pick

    key_block = min(length, 256)
    cross_rows = S * window
    cross_step = min(cross_rows, 384)
    wait_all(CAND, recv_c, window)
    for row in range(0, cross_rows, cross_step):
        rows = slice(row, row + cross_step)
        queries = recv_c[rows]
        total = jnp.zeros((cross_step, W), F32)
        for t in range(heads_here):
            for col in range(0, length, key_block):
                cols = slice(col, col + key_block)
                weights = silu_half(dot(queries, key_heads[t, cols], ((1,), (1,))))
                total = total + dot(weights.astype(BF16), value_heads[t, cols])
        cross_ref[rows] = total.astype(BF16)

    def give_back(phase, src, dst, rows, other):
        source = src.at[pl.ds(other * rows, rows), :]

        @pl.when(other != me)
        def _():
            remote(phase, source, dst.at[pl.ds(me * rows, rows), :], other).start()

    for other in range(S):
        give_back(CROSS, cross_ref, back_c_ref, window, other)
    mine = pl.ds(pl.multiple_of(me * window, ROW_TILE), window)
    back_c_ref[mine, :] = cross_ref[mine, :]

    wait_all(QUERY, recv_q, tokens)
    row_ids = lax.broadcasted_iota(jnp.int32, (key_block, key_block), 0)
    col_ids = lax.broadcasted_iota(jnp.int32, (key_block, key_block), 1)
    done = 0
    for row in range(0, length, key_block):
        rows = slice(row, row + key_block)
        queries = recv_q[rows]
        total = jnp.zeros((key_block, W), F32)
        for t in range(heads_here):
            for col in range(0, row + 1, key_block):
                cols = slice(col, col + key_block)
                weights = silu_half(dot(queries, key_heads[t, cols], ((1,), (1,))))
                if col == row:
                    weights = jnp.where(col_ids <= row_ids, weights, 0.0)
                total = total + dot(weights.astype(BF16), value_heads[t, cols])
        att_ref[rows] = total.astype(BF16)
        while (done + 1) * tokens <= row + key_block:
            give_back(BACK, att_ref, back_ref, tokens, done)
            done += 1
    mine = pl.ds(pl.multiple_of(me * tokens, ROW_TILE), tokens)
    back_ref[mine, :] = att_ref[mine, :]

    gain_attn = gain_attn_ref[...]
    out_copy.wait()

    def gather_rows(ref, rows, n):
        parts = [
            ref[(n * blocks + block) * rows : (n * blocks + block + 1) * rows, :]
            for block in range(blocks)
        ]
        return jnp.concatenate(parts, axis=1)

    def project_out(normed, base):
        return (base + dot(normed, wo_buf[...])).astype(BF16)

    wait_all(CROSS, back_c_ref, window)
    windows = jnp.concatenate([gather_rows(back_c_ref, window, n) for n in range(hists)], axis=0)
    cross = dot(picks, windows, ((0,), (0,)))
    cand_gated = (rms_apply(cross, gain_attn) * cand_gate_ref[...].astype(F32)).astype(BF16)
    cand_out_ref[...] = project_out(cand_gated, cand_ref[...].astype(F32))

    wait_all(BACK, back_ref, tokens)
    for n in range(hists):
        attended = gather_rows(back_ref, tokens, n).astype(F32)
        gate = gate_ref[n * tokens : (n + 1) * tokens].astype(F32)
        gated = (rms_apply(attended, gain_attn) * gate).astype(BF16)
        hist_out_ref[n] = project_out(gated, hist_ref[n].astype(F32))

    for copy in sent:
        copy.wait_send()
    for step in range(1, S):
        other = lax.rem(me + step, S)
        for phase, src, dst, rows in (
            (CROSS, cross_ref, back_c_ref, window),
            (BACK, att_ref, back_ref, tokens),
        ):
            source = src.at[pl.ds(other * rows, rows), :]
            remote(phase, source, dst.at[pl.ds(me * rows, rows), :], other).wait_send()


def per_device(history, candidates, lengths, assignment, weight_in, weight_out, gain_in, gain_attn):
    S = lax.axis_size("seq")
    hists, tokens, width = history.shape
    cands = candidates.shape[1]
    heads_here = hists * H // S
    W = heads_here * (width // H)
    length = tokens * S
    window = -(-CAP // ROW_TILE) * ROW_TILE
    rows = hists * tokens
    vmem = pl.BlockSpec(memory_space=pltpu.VMEM)
    smem = pl.BlockSpec(memory_space=pltpu.SMEM)
    hbm = pl.BlockSpec(memory_space=pl.ANY)

    def buf(*shape):
        return pltpu.VMEM(shape, BF16)

    history_out, candidate_out = pl.pallas_call(
        functools.partial(layer_kernel, S),
        out_shape=(
            jax.ShapeDtypeStruct(history.shape, BF16),
            jax.ShapeDtypeStruct((cands, width), BF16),
        ),
        in_specs=[smem, vmem, vmem, vmem, vmem, vmem, hbm, hbm],
        out_specs=(vmem, vmem),
        scratch_shapes=[
            buf(4, width, width),
            buf(width, width),
            buf(rows, width),
            buf(rows, width),
            buf(cands, width),
            buf(3, S, tokens, W),
            buf(S, window, W),
            buf(length, W),
            buf(length, W),
            buf(length, W),
            buf(S * window, W),
            buf(heads_here, length, W),
            buf(heads_here, length, W),
            buf(length, W),
            buf(S * window, W),
            buf(length, W),
            buf(S * window, W),
            pltpu.SemaphoreType.DMA((5,)),
            pltpu.SemaphoreType.DMA((6, S)),
            pltpu.SemaphoreType.DMA((6, S)),
        ],
        compiler_params=pltpu.CompilerParams(
            collective_id=0, has_side_effects=True, vmem_limit_bytes=60 * 1024 * 1024
        ),
        name="gated_layer",
    )(
        lengths,
        history,
        candidates[0],
        assignment,
        gain_in[None],
        gain_attn[None],
        weight_in,
        weight_out,
    )
    return (history_out, candidate_out[None])


def solution(mesh):
    in_specs = (
        P(("groups", "dp"), "seq", None),
        P(("groups", "dp"), "seq", None),
        P(("groups", "dp")),
        P(("groups", "dp"), "seq"),
        P(),
        P(),
        P(),
        P(),
    )
    out_specs = (P(("groups", "dp"), "seq", None), P(("groups", "dp"), "seq", None))
    return jax.shard_map(
        per_device, mesh=mesh, in_specs=in_specs, out_specs=out_specs, check_vma=False
    )
```

time: 201 us -> 55.7 us (0.28); the launches traced: 199 us -> 55.5 us
  local copies, waits for them, and re-layouts: 74.7 us -> 3.33 us
  Pallas kernels: 0 us -> 51.5 us
  matrix products: 37.3 us -> 0 us
  other arithmetic: 36.8 us -> 0 us
  starting transfers between devices: 33.6 us -> 0 us
  waiting for transfers between devices: 14.4 us -> 0 us
    pallas_call x0 -> x1, Pallas kernels: none -> 51.5 us  [per_device(): pl.pallas_call(functools.partial(layer_kernel, S), out_shape=(jax.ShapeDt...]
    dot_general x36 -> x0, matrix products: 37.3 us -> none  [the longest x12 15.2 us: query_part(): jnp.dot(weights, values, preferred_element_type=jnp.float32)]
    all_to_all x6 -> x0, starting transfers between devices: 33.6 us -> none  [the longest x1 7.31 us: per_device(): lax.all_to_all(outgoing, 'seq', split_axis=0, concat_axis=1, tiled=True)]
    dynamic_slice x28 -> x0, local copies, waits for them, and re-layouts: 20.1 us -> none  [the longest x12 8.53 us: per_device(): lax.map(self_item, (heads_query, heads_keys, heads_values, item_valid))]
    lt x32 -> x0, other arithmetic: 19.6 us -> none  [the longest x20 12.7 us: cand_part(): key_positions[None, :] < valid]
    all_to_all x6 -> x0, waiting for transfers between devices: 14.4 us -> none  [the longest x1 7.85 us: per_device(): lax.all_to_all(to_items(keys), 'seq', split_axis=0, concat_axis=1, tiled=...]
    all_to_all x12 -> x0, local copies, waits for them, and re-layouts: 14.1 us -> none  [the longest x2 2.82 us: per_device(): lax.all_to_all(attended.reshape(items_local, length * HD), 'seq', split_a...]
    add x14 -> x0, other arithmetic: 9.16 us -> none  [the longest x12 8.29 us: query_part(): row_positions = first_row + jnp.arange(block_rows, dtype=jnp.int32)]
  transfers between devices with their start and end apart: 6 -> 0, of which waited for: 3 -> 0; matrix products, arithmetic and copies ran while one was open for 60% -> 0% of each run, Pallas kernels for 0% -> 0%
where the time goes in v1:
time: 55.7 us; the launch traced here: 55.5 us
  Pallas kernels  51.5 us (92%)
  local copies, waits for them, and re-layouts  3.33 us (6%)
  between operations  0.64 us (1%)
    pallas_call x1, Pallas kernels, per_device(): pl.pallas_call(functools.partial(layer_kernel, S), out_shape=(jax.ShapeDt...  51.5 us
    unnamed x2, local copies, waits for them, and re-layouts  3.33 us

profile of v1, /device:TPU:0, one launch (start us, length us, event | category | flops | bytes accessed | tf_op | source)
XLA Modules:
  0.0 55.5 jit_solution(3925184841763506687)
XLA Ops:
  0.6 51.5 %gated_layer.1 = (bf16[2,96,1024]{2,1,0:T(8,128)(2,1)}, bf16[64,1024]{1,0:T(8,128)(2,1)}) custom-call(s32[2]{0:T(128)} %len_ref.1, bf16[2,96,1024]{2,1,0:T(8,128)(2,1)} %hist_ref.1, bf16[64,1024]{1,0:T(8,128)(2,1)} %bitcast.4, s32[1,64]{1,0:T(1,128)} %owner_ref.1, f32[1,1024]{1,0:T(1,128)} %bitcast.6, f32[1,1024]{1,0:T(1,128)} %bitcast.7, ...), custom_call_target="tpu_custom_call" | custom-call | tf_op jit(solution)/shard_map/gated_layer/pallas_call | solution.py:303
  52.2 1.8 %copy.12 = bf16[2,96,1024]{2,1,0:T(8,128)(2,1)} copy(bf16[2,96,1024]{2,1,0:T(8,128)(2,1)} %get-tuple-element.8) | data formatting | bytes 786432
  53.9 1.6 %copy.13 = bf16[1,64,1024]{2,1,0:T(8,128)(2,1)} copy(bf16[1,64,1024]{2,1,0:T(8,128)(2,1)} %bitcast.5) | data formatting | bytes 262144

commit v2 on v1

--- a/solution.py
+++ b/solution.py
@@ -13,7 +13,7 @@
 MESH = pl.DeviceIdType.MESH
 F32 = jnp.float32
 BF16 = jnp.bfloat16
-KEY, VALUE, CAND, QUERY, BACK, CROSS = range(6)
+KEY, VALUE, CAND, QUERY, BACK, CROSS, ROWS = range(7)
 
 
 def dot(a, b, dims=((1,), (0,))):
@@ -43,6 +43,7 @@
     w_buf,
     wo_buf,
     normed_ref,
+    swap_ref,
     gate_ref,
     cand_gate_ref,
     send_kvq,
@@ -72,6 +73,7 @@
     window = recv_c.shape[0] // S
     length = tokens * S
     my_hist = me // blocks
+    place_in_half = lax.rem(me, blocks)
 
     def weight_copy(part):
         return pltpu.make_async_copy(
@@ -128,22 +130,49 @@
             copy.start()
             sent.append(copy)
 
-    def project_and_send(phase, part, slot, dst):
-        normed = normed_ref[...]
+    def swap(step):
+        other_hist = lax.rem(my_hist + step, hists)
+        return pltpu.make_async_remote_copy(
+            src_ref=hist_ref.at[other_hist],
+            dst_ref=swap_ref.at[my_hist],
+            send_sem=send_sem.at[ROWS, other_hist],
+            recv_sem=recv_sem.at[ROWS, my_hist],
+            device_id={"seq": other_hist * blocks + place_in_half},
+            device_id_type=MESH,
+        )
+
+    def project_and_send(phase, part, slot, dst, normed, half):
         for first in range(0, width, chunk):
             value = dot(normed, w_buf[part, :, first : first + chunk]).astype(BF16)
             for block, piece in blocks_of(first, value):
-                for n in range(hists):
-                    send_kvq[slot, n * blocks + block] = piece[n * tokens : (n + 1) * tokens]
-        if phase == KEY:
-            pl.semaphore_wait(barrier, S - 1)
-        scatter(phase, lambda other: send_kvq.at[slot, other], dst, tokens)
-        dst[pl.ds(pl.multiple_of(me * tokens, ROW_TILE), tokens), :] = send_kvq[slot, me]
-
+                send_kvq[slot, half * blocks + block] = piece
+        shard = half * blocks + place_in_half
+        to = dst.at[pl.ds(pl.multiple_of(shard * tokens, ROW_TILE), tokens), :]
+        for step in range(1, blocks):
+            block = lax.rem(place_in_half + step, blocks)
+            copy = pltpu.make_async_remote_copy(
+                src_ref=send_kvq.at[slot, half * blocks + block],
+                dst_ref=to,
+                send_sem=send_sem.at[phase, half * blocks + block],
+                recv_sem=recv_sem.at[phase, shard],
+                device_id={"seq": my_hist * blocks + block},
+                device_id_type=MESH,
+            )
+            copy.start()
+            sent.append(copy)
+        to[...] = send_kvq[slot, half * blocks + place_in_half]
+
+    pl.semaphore_wait(barrier, S - 1)
+    for step in range(1, hists):
+        copy = swap(step)
+        copy.start()
+        sent.append(copy)
+
+    own = normed_ref[pl.ds(pl.multiple_of(my_hist * tokens, ROW_TILE), tokens), :]
     weight_copy(2).wait()
-    project_and_send(KEY, 2, 0, recv_k)
+    project_and_send(KEY, 2, 0, recv_k, own, my_hist)
     weight_copy(3).wait()
-    project_and_send(VALUE, 3, 1, recv_v)
+    project_and_send(VALUE, 3, 1, recv_v, own, my_hist)
 
     cand_rows = cand_ref[...].astype(F32)
     cand_normed = rms_apply(cand_rows, gain_in).astype(BF16)
@@ -170,7 +199,7 @@
                 send_c[n * blocks + block] = piece[n * window : (n + 1) * window]
     scatter(CAND, lambda other: send_c.at[other], recv_c, window)
     recv_c[pl.ds(pl.multiple_of(me * window, ROW_TILE), window), :] = send_c[me]
-    project_and_send(QUERY, 1, 2, recv_q)
+    project_and_send(QUERY, 1, 2, recv_q, own, my_hist)
 
     weight_copy(0).wait()
     for first in range(0, width, chunk):
@@ -183,13 +212,45 @@
         for step in range(1, S):
             arrival(phase, ref, rows, lax.rem(me + S - step, S)).wait_recv()
 
+    for step in range(1, hists):
+        half = lax.rem(my_hist + step, hists)
+        here = swap_ref.at[half]
+        pltpu.make_async_remote_copy(
+            src_ref=here,
+            dst_ref=here,
+            send_sem=send_sem.at[ROWS, half],
+            recv_sem=recv_sem.at[ROWS, half],
+            device_id={"seq": half * blocks + place_in_half},
+            device_id_type=MESH,
+        ).wait_recv()
+        theirs = rms_apply(swap_ref[half].astype(F32), gain_in).astype(BF16)
+        project_and_send(KEY, 2, 0, recv_k, theirs, half)
+        project_and_send(VALUE, 3, 1, recv_v, theirs, half)
+        project_and_send(QUERY, 1, 2, recv_q, theirs, half)
+
+    def wait_shards(phase, ref):
+        for turn in range(hists):
+            half = lax.rem(my_hist + turn, hists)
+            for step in range(1, blocks):
+                source = lax.rem(place_in_half + blocks - step, blocks)
+                shard = half * blocks + source
+                here = ref.at[pl.ds(pl.multiple_of(shard * tokens, ROW_TILE), tokens), :]
+                pltpu.make_async_remote_copy(
+                    src_ref=here,
+                    dst_ref=here,
+                    send_sem=send_sem.at[phase, shard],
+                    recv_sem=recv_sem.at[phase, shard],
+                    device_id={"seq": my_hist * blocks + source},
+                    device_id_type=MESH,
+                ).wait_recv()
+
     lane_head = lax.broadcasted_iota(jnp.int32, (1, W), 1) // head_dim
     score_half = 0.5 * head_dim ** (-0.5)
-    wait_all(KEY, recv_k, tokens)
+    wait_shards(KEY, recv_k)
     for t in range(heads_here):
         pick = jnp.where(lane_head == t, score_half, 0.0).astype(BF16)
         key_heads[t] = recv_k[...] * pick
-    wait_all(VALUE, recv_v, tokens)
+    wait_shards(VALUE, recv_v)
     valid = len_ref[my_hist]
     inside = (lax.broadcasted_iota(jnp.int32, (length, W), 0) < valid).astype(F32).astype(BF16)
     values = recv_v[...] * inside
@@ -224,7 +285,7 @@
     mine = pl.ds(pl.multiple_of(me * window, ROW_TILE), window)
     back_c_ref[mine, :] = cross_ref[mine, :]
 
-    wait_all(QUERY, recv_q, tokens)
+    wait_shards(QUERY, recv_q)
     row_ids = lax.broadcasted_iota(jnp.int32, (key_block, key_block), 0)
     col_ids = lax.broadcasted_iota(jnp.int32, (key_block, key_block), 1)
     done = 0
@@ -312,6 +373,7 @@
             buf(4, width, width),
             buf(width, width),
             buf(rows, width),
+            buf(hists, tokens, width),
             buf(rows, width),
             buf(cands, width),
             buf(3, S, tokens, W),
@@ -327,8 +389,8 @@
             buf(length, W),
             buf(S * window, W),
             pltpu.SemaphoreType.DMA((5,)),
-            pltpu.SemaphoreType.DMA((6, S)),
-            pltpu.SemaphoreType.DMA((6, S)),
+            pltpu.SemaphoreType.DMA((7, S)),
+            pltpu.SemaphoreType.DMA((7, S)),
         ],
         compiler_params=pltpu.CompilerParams(
             collective_id=0, has_side_effects=True, vmem_limit_bytes=60 * 1024 * 1024

time: 55.7 us -> 47.3 us (0.85)
  Pallas kernels: 51.5 us -> 43.2 us
    pallas_call x1, Pallas kernels: 51.5 us -> 43.2 us  [per_device(): pl.pallas_call(functools.partial(layer_kernel, S), out_shape=(jax.ShapeDt...]
where the time goes in v2:
time: 47.3 us; the launch traced here: 47.1 us
  Pallas kernels  43.2 us (91%)
  local copies, waits for them, and re-layouts  3.33 us (7%)
  between operations  0.64 us (1%)
    pallas_call x1, Pallas kernels, per_device(): pl.pallas_call(functools.partial(layer_kernel, S), out_shape=(jax.ShapeDt...  43.2 us
    unnamed x2, local copies, waits for them, and re-layouts  3.33 us

profile of v2, /device:TPU:0, one launch (start us, length us, event | category | flops | bytes accessed | tf_op | source)
XLA Modules:
  0.0 47.1 jit_solution(6980621796242557828)
XLA Ops:
  0.6 43.2 %gated_layer.1 = (bf16[2,96,1024]{2,1,0:T(8,128)(2,1)}, bf16[64,1024]{1,0:T(8,128)(2,1)}) custom-call(s32[2]{0:T(128)} %len_ref.1, bf16[2,96,1024]{2,1,0:T(8,128)(2,1)} %hist_ref.1, bf16[64,1024]{1,0:T(8,128)(2,1)} %bitcast.4, s32[1,64]{1,0:T(1,128)} %owner_ref.1, f32[1,1024]{1,0:T(1,128)} %bitcast.6, f32[1,1024]{1,0:T(1,128)} %bitcast.7, ...), custom_call_target="tpu_custom_call" | custom-call | tf_op jit(solution)/shard_map/gated_layer/pallas_call | solution.py:364
  43.8 1.8 %copy.12 = bf16[2,96,1024]{2,1,0:T(8,128)(2,1)} copy(bf16[2,96,1024]{2,1,0:T(8,128)(2,1)} %get-tuple-element.8) | data formatting | bytes 786432
  45.6 1.6 %copy.13 = bf16[1,64,1024]{2,1,0:T(8,128)(2,1)} copy(bf16[1,64,1024]{2,1,0:T(8,128)(2,1)} %bitcast.5) | data formatting | bytes 262144
